TPU v7x, 32 devices: a whole 2x2x4 slice. The times are simulated.
32 devices in a mesh: row: 8 (over y, x, core), col: 4 (over z).
Axes of the slice: x: 2, y: 2, z: 4, core: 2. Of those that a mesh axis runs over, the one named last changes fastest.
Arguments:
- pair_state: bfloat16 [128, 128, 128], P('row', 'col'), may hold values from -6 to 6
- pair_mask: int32 [128, 128], P('row', 'col'), may hold values 0 or 1
- input_gain: float32 [2, 128], replicated, may hold values from 0.25 to 1.75
- input_bias: float32 [2, 128], replicated, may hold values from -1.5 to 1.5
- proj_weights: bfloat16 [2, 128, 512], replicated, may hold values from -0.5 to 0.5
- gate_weights: bfloat16 [2, 128, 128], replicated, may hold values from -0.5 to 0.5
- output_gain: float32 [2, 128], replicated, may hold values from 0.25 to 1.75
- output_bias: float32 [2, 128], replicated, may hold values from -1.5 to 1.5
- output_weights: bfloat16 [2, 128, 128], replicated, may hold values from -0.5 to 0.5
Outputs:
- pair_out: bfloat16 [128, 128, 128], P('row', 'col')
All inputs are finite; a program needn't handle non-finite values. No bound on the sum of `pair_mask` on one device may be relied on, other than what follows from the above.
Results may differ from a plain program's by a relative error of at most 0.0058.
Values may be sent and summed in bfloat16 or wider, within the bound.
A program may use at most 64 MiB of HBM per device.

v0:
```python
import jax
import jax.numpy as jnp
from jax import lax
from jax.sharding import PartitionSpec as P

epsilon = 1e-05


def normalize(values, weight_scale, weight_shift, reduce_axis):
    average = jnp.mean(values, axis=reduce_axis, keepdims=True)
    centred = values - average
    spread = jnp.mean(centred * centred, axis=reduce_axis, keepdims=True)
    return centred * lax.rsqrt(spread + epsilon) * weight_scale + weight_shift


def contract(left_panel, right_panel, layer_index):
    if layer_index == 0:
        product = jnp.einsum(
            "cik,cjk->cij", left_panel, right_panel, preferred_element_type=jnp.float32
        )
    else:
        product = jnp.einsum(
            "cki,ckj->cij", left_panel, right_panel, preferred_element_type=jnp.float32
        )
    return product.astype(jnp.bfloat16)


def gated_panel(pair_ln, weights, first, hidden, mask_float):
    projected = jnp.einsum(
        "ijd,de->eij",
        pair_ln,
        weights[:, first : first + 2 * hidden],
        preferred_element_type=jnp.float32,
    )
    return (jax.nn.sigmoid(projected[:hidden]) * projected[hidden:] * mask_float).astype(
        jnp.bfloat16
    )


def on_device(
    pair_state,
    pair_mask,
    input_gain,
    input_bias,
    proj_weights,
    gate_weights,
    output_gain,
    output_bias,
    output_weights,
):
    tile_rows, tile_cols, channels = pair_state.shape
    hidden = output_weights.shape[1]
    row_count = lax.axis_size("row")
    col_count = lax.axis_size("col")
    per_device = hidden // (row_count * col_count)
    current = pair_state.astype(jnp.float32)
    mask_float = pair_mask.astype(jnp.float32)[None]
    for layer_index in range(2):
        pair_ln = normalize(current, input_gain[layer_index], input_bias[layer_index], -1).astype(
            jnp.bfloat16
        )
        left_panel = gated_panel(pair_ln, proj_weights[layer_index], 0, hidden, mask_float)
        right_panel = gated_panel(
            pair_ln, proj_weights[layer_index], 2 * hidden, hidden, mask_float
        )
        gate_value = jax.nn.sigmoid(
            jnp.einsum(
                "ijd,de->ije",
                pair_ln,
                gate_weights[layer_index],
                preferred_element_type=jnp.float32,
            )
        )
        scale_out = output_gain[layer_index]
        shift_out = output_bias[layer_index]
        weight_out = output_weights[layer_index]
        left_recv, right_recv = (
            lax.all_to_all(left_panel, ("row", "col"), split_axis=0, concat_axis=1, tiled=True),
            lax.all_to_all(right_panel, ("row", "col"), split_axis=0, concat_axis=1, tiled=True),
        )
        left_chan = (
            left_recv.reshape(per_device, row_count, col_count, tile_rows, tile_cols)
            .transpose(0, 1, 3, 2, 4)
            .reshape(per_device, row_count * tile_rows, col_count * tile_cols)
        )
        right_chan = (
            right_recv.reshape(per_device, row_count, col_count, tile_rows, tile_cols)
            .transpose(0, 1, 3, 2, 4)
            .reshape(per_device, row_count * tile_rows, col_count * tile_cols)
        )
        product = contract(left_chan, right_chan, layer_index)
        arranged = (
            product.reshape(per_device, row_count, tile_rows, col_count, tile_cols)
            .transpose(0, 1, 3, 2, 4)
            .reshape(per_device, row_count * col_count * tile_rows, tile_cols)
        )
        returned = lax.all_to_all(arranged, ("row", "col"), split_axis=1, concat_axis=0, tiled=True)
        normed = normalize(
            returned.astype(jnp.float32), scale_out[:, None, None], shift_out[:, None, None], 0
        ).astype(jnp.bfloat16)
        update = jnp.einsum("cij,cd->ijd", normed, weight_out, preferred_element_type=jnp.float32)
        current = current + gate_value * update
    return current.astype(jnp.bfloat16)


def solution(mesh):
    return jax.shard_map(
        on_device,
        mesh=mesh,
        in_specs=(P("row", "col", None), P("row", "col"), P(), P(), P(), P(), P(), P(), P()),
        out_specs=P("row", "col", None),
        check_vma=False,
    )
```

profile of v0, /device:TPU:0, one launch (start us, length us, event | category | flops | bytes accessed | tf_op | source)
XLA Modules:
  0.0 89.4 jit_solution(1985467403986894677)
XLA Ops:
  0.0 1.1 %convert_reduce_fusion = f32[16,32]{1,0:T(8,128)S(1)} fusion(bf16[16,32,128]{2,1,0:T(8,128)(2,1)} %param.9), kind=kLoop, calls=%fused_computation.44 | loop fusion | flops 130560 | bytes 133120 | tf_op jit(solution)/shard_map/reduce_sum | solution.py:10
  1.4 1.0 %slice_bitcast_fusion = (bf16[128,512]{1,0:T(8,128)(2,1)S(1)}, bf16[128,512]{1,0:T(8,128)(2,1)S(1)}) fusion(bf16[2,128,512]{2,1,0:T(8,128)(2,1)} %param.13), kind=kLoop, calls=%fused_computation.81 | loop fusion | bytes 524288 | tf_op jit(solution)/shard_map/squeeze | solution.py:62
  4.1 1.2 %reshape.155 = bf16[32,2,1024]{2,1,0:T(2,128)(2,1)} reshape(bf16[128,16,32]{2,1,0:T(8,128)(2,1)S(1)} %copy.33) | data formatting | bytes 262144
  5.3 7.3 %all-to-all-start = ((bf16[32,2,1024]{2,1,0:T(2,128)(2,1)}), bf16[32,2,1024]{2,1,0:T(2,128)(2,1)S(1)}, u32[]{:S(2)}, u32[]{:S(2)}) async-start(bf16[32,2,1024]{2,1,0:T(2,128)(2,1)} %reshape.155), calls=%async_computation | async-start | bytes 262144 | tf_op jit(solution)/shard_map/all_to_all | solution.py:78
  12.6 0.4 copy.35
  13.1 1.2 %reshape.157 = bf16[32,2,1024]{2,1,0:T(2,128)(2,1)} reshape(bf16[128,16,32]{2,1,0:T(8,128)(2,1)S(1)} %copy.35) | data formatting | bytes 262144
  14.2 6.8 %all-to-all-done = bf16[32,2,1024]{2,1,0:T(2,128)(2,1)S(1)} async-done(((bf16[32,2,1024]{2,1,0:T(2,128)(2,1)}), bf16[32,2,1024]{2,1,0:T(2,128)(2,1)S(1)}, u32[]{:S(2)}, u32[]{:S(2)}) %all-to-all-start) | async-done | bytes 131104 | tf_op jit(solution)/shard_map/all_to_all | solution.py:78
  21.0 2.6 %all-to-all-start.1 = ((bf16[32,2,1024]{2,1,0:T(2,128)(2,1)}), bf16[32,2,1024]{2,1,0:T(2,128)(2,1)S(1)}, u32[]{:S(2)}, u32[]{:S(2)}) async-start(bf16[32,2,1024]{2,1,0:T(2,128)(2,1)} %reshape.157), calls=%async_computation.1 | async-start | bytes 262144 | tf_op jit(solution)/shard_map/all_to_all | solution.py:79
  24.6 7.4 %all-to-all-done.1 = bf16[32,2,1024]{2,1,0:T(2,128)(2,1)S(1)} async-done(((bf16[32,2,1024]{2,1,0:T(2,128)(2,1)}), bf16[32,2,1024]{2,1,0:T(2,128)(2,1)S(1)}, u32[]{:S(2)}, u32[]{:S(2)}) %all-to-all-start.1) | async-done | bytes 131104 | tf_op jit(solution)/shard_map/all_to_all | solution.py:79
  33.9 1.2 %reshape.159 = bf16[32,2,1024]{2,1,0:T(2,128)(2,1)} reshape(bf16[512,4,32]{2,1,0:T(4,128)(2,1)S(1)} %bitcast.161) | data formatting | bytes 262144
  35.1 2.7 %all-to-all-start.2 = ((bf16[32,2,1024]{2,1,0:T(2,128)(2,1)}), bf16[32,2,1024]{2,1,0:T(2,128)(2,1)S(1)}, u32[]{:S(2)}, u32[]{:S(2)}) async-start(bf16[32,2,1024]{2,1,0:T(2,128)(2,1)} %reshape.159), calls=%async_computation.2 | async-start | bytes 262144 | tf_op jit(solution)/shard_map/all_to_all | solution.py:97
  38.2 0.4 copy-done.7
  39.0 7.2 %all-to-all-done.2 = bf16[32,2,1024]{2,1,0:T(2,128)(2,1)S(1)} async-done(((bf16[32,2,1024]{2,1,0:T(2,128)(2,1)}), bf16[32,2,1024]{2,1,0:T(2,128)(2,1)S(1)}, u32[]{:S(2)}, u32[]{:S(2)}) %all-to-all-start.2) | async-done | bytes 131104 | tf_op jit(solution)/shard_map/all_to_all | solution.py:97
  47.4 0.8 copy-done.1
  50.1 1.2 %reshape.161 = bf16[32,2,1024]{2,1,0:T(2,128)(2,1)} reshape(bf16[128,16,32]{2,1,0:T(8,128)(2,1)S(1)} %copy.44) | data formatting | bytes 262144
  51.2 2.6 %all-to-all-start.3 = ((bf16[32,2,1024]{2,1,0:T(2,128)(2,1)}), bf16[32,2,1024]{2,1,0:T(2,128)(2,1)S(1)}, u32[]{:S(2)}, u32[]{:S(2)}) async-start(bf16[32,2,1024]{2,1,0:T(2,128)(2,1)} %reshape.161), calls=%async_computation.3 | async-start | bytes 262144 | tf_op jit(solution)/shard_map/all_to_all | solution.py:78
  54.3 1.2 %reshape.163 = bf16[32,2,1024]{2,1,0:T(2,128)(2,1)} reshape(bf16[128,16,32]{2,1,0:T(8,128)(2,1)S(1)} %copy.46) | data formatting | bytes 262144
  55.4 6.8 %all-to-all-done.3 = bf16[32,2,1024]{2,1,0:T(2,128)(2,1)S(1)} async-done(((bf16[32,2,1024]{2,1,0:T(2,128)(2,1)}), bf16[32,2,1024]{2,1,0:T(2,128)(2,1)S(1)}, u32[]{:S(2)}, u32[]{:S(2)}) %all-to-all-start.3) | async-done | bytes 131104 | tf_op jit(solution)/shard_map/all_to_all | solution.py:78
  62.2 2.7 %all-to-all-start.4 = ((bf16[32,2,1024]{2,1,0:T(2,128)(2,1)}), bf16[32,2,1024]{2,1,0:T(2,128)(2,1)S(1)}, u32[]{:S(2)}, u32[]{:S(2)}) async-start(bf16[32,2,1024]{2,1,0:T(2,128)(2,1)} %reshape.163), calls=%async_computation.4 | async-start | bytes 262144 | tf_op jit(solution)/shard_map/all_to_all | solution.py:79
  65.9 7.2 %all-to-all-done.4 = bf16[32,2,1024]{2,1,0:T(2,128)(2,1)S(1)} async-done(((bf16[32,2,1024]{2,1,0:T(2,128)(2,1)}), bf16[32,2,1024]{2,1,0:T(2,128)(2,1)S(1)}, u32[]{:S(2)}, u32[]{:S(2)}) %all-to-all-start.4) | async-done | bytes 131104 | tf_op jit(solution)/shard_map/all_to_all | solution.py:79
  75.1 1.2 %reshape.165 = bf16[32,2,1024]{2,1,0:T(2,128)(2,1)} reshape(bf16[512,4,32]{2,1,0:T(4,128)(2,1)S(1)} %bitcast.166) | data formatting | bytes 262144
  76.3 2.6 %all-to-all-start.5 = ((bf16[32,2,1024]{2,1,0:T(2,128)(2,1)}), bf16[32,2,1024]{2,1,0:T(2,128)(2,1)S(1)}, u32[]{:S(2)}, u32[]{:S(2)}) async-start(bf16[32,2,1024]{2,1,0:T(2,128)(2,1)} %reshape.165), calls=%async_computation.5 | async-start | bytes 262144 | tf_op jit(solution)/shard_map/all_to_all | solution.py:97
  79.5 7.8 %all-to-all-done.5 = bf16[32,2,1024]{2,1,0:T(2,128)(2,1)S(1)} async-done(((bf16[32,2,1024]{2,1,0:T(2,128)(2,1)}), bf16[32,2,1024]{2,1,0:T(2,128)(2,1)S(1)}, u32[]{:S(2)}, u32[]{:S(2)}) %all-to-all-start.5) | async-done | bytes 131104 | tf_op jit(solution)/shard_map/all_to_all | solution.py:97
  88.4 1.0 %fusion.8 = bf16[16,32,128]{2,1,0:T(8,128)(2,1)} fusion(f32[16,32,128]{2,1,0:T(8,128)S(1)} %get-tuple-element.20, f32[16,32,128]{2,1,0:T(8,128)S(1)} %fusion.4, bf16[128,16,32]{2,1,0:T(8,128)(2,1)S(1)} %bitcast.156, bf16[2,128,128]{2,1,0:T(8,128)(2,1)S(1)} %copy-done.1), kind=kOutput, calls=%fused_computation.16 | convolution fusion | flops 16973824 | bytes 1212416 | tf_op jit(solution)/shard_map/cij,cd->ijd/dot_general | solution.py:101
  (80 shorter events, 13.4 us)
Async XLA Ops:
  0.0 1.1 %copy-start = (bf16[16,32,128]{2,1,0:T(8,128)(2,1)S(1)}, bf16[16,32,128]{2,1,0:T(8,128)(2,1)}, u32[]{:S(2)}) copy-start(bf16[16,32,128]{2,1,0:T(8,128)(2,1)} %param.9) | copy-start | bytes 393220
  1.4 1.0 %copy-start.3 = (f32[2,128]{1,0:T(2,128)S(1)}, f32[2,128]{1,0:T(2,128)}, u32[]{:S(2)}) copy-start(f32[2,128]{1,0:T(2,128)} %param.12) | copy-start | bytes 3076
  1.4 1.0 %copy-start.4 = (f32[2,128]{1,0:T(2,128)S(1)}, f32[2,128]{1,0:T(2,128)}, u32[]{:S(2)}) copy-start(f32[2,128]{1,0:T(2,128)} %param.11) | copy-start | bytes 3076
  2.8 0.7 copy-start.2
  5.3 15.7 %all-to-all-start = ((bf16[32,2,1024]{2,1,0:T(2,128)(2,1)}), bf16[32,2,1024]{2,1,0:T(2,128)(2,1)S(1)}, u32[]{:S(2)}, u32[]{:S(2)}) async-start(bf16[32,2,1024]{2,1,0:T(2,128)(2,1)} %reshape.155), calls=%async_computation | async-start | bytes 262144 | tf_op jit(solution)/shard_map/all_to_all | solution.py:78
  21.0 11.0 %all-to-all-start.1 = ((bf16[32,2,1024]{2,1,0:T(2,128)(2,1)}), bf16[32,2,1024]{2,1,0:T(2,128)(2,1)S(1)}, u32[]{:S(2)}, u32[]{:S(2)}) async-start(bf16[32,2,1024]{2,1,0:T(2,128)(2,1)} %reshape.157), calls=%async_computation.1 | async-start | bytes 262144 | tf_op jit(solution)/shard_map/all_to_all | solution.py:79
  35.1 2.7 %copy-start.5 = (f32[2,128]{1,0:T(2,128)S(1)}, f32[2,128]{1,0:T(2,128)}, u32[]{:S(2)}) copy-start(f32[2,128]{1,0:T(2,128)} %param.16) | copy-start | bytes 3076
  35.1 2.7 %copy-start.6 = (f32[2,128]{1,0:T(2,128)S(1)}, f32[2,128]{1,0:T(2,128)}, u32[]{:S(2)}) copy-start(f32[2,128]{1,0:T(2,128)} %param.15) | copy-start | bytes 3076
  35.1 11.1 %all-to-all-start.2 = ((bf16[32,2,1024]{2,1,0:T(2,128)(2,1)}), bf16[32,2,1024]{2,1,0:T(2,128)(2,1)S(1)}, u32[]{:S(2)}, u32[]{:S(2)}) async-start(bf16[32,2,1024]{2,1,0:T(2,128)(2,1)} %reshape.159), calls=%async_computation.2 | async-start | bytes 262144 | tf_op jit(solution)/shard_map/all_to_all | solution.py:97
  37.8 0.8 copy-start.7
  47.3 0.8 copy-start.1
  51.2 11.0 %all-to-all-start.3 = ((bf16[32,2,1024]{2,1,0:T(2,128)(2,1)}), bf16[32,2,1024]{2,1,0:T(2,128)(2,1)S(1)}, u32[]{:S(2)}, u32[]{:S(2)}) async-start(bf16[32,2,1024]{2,1,0:T(2,128)(2,1)} %reshape.161), calls=%async_computation.3 | async-start | bytes 262144 | tf_op jit(solution)/shard_map/all_to_all | solution.py:78
  62.2 11.0 %all-to-all-start.4 = ((bf16[32,2,1024]{2,1,0:T(2,128)(2,1)}), bf16[32,2,1024]{2,1,0:T(2,128)(2,1)S(1)}, u32[]{:S(2)}, u32[]{:S(2)}) async-start(bf16[32,2,1024]{2,1,0:T(2,128)(2,1)} %reshape.163), calls=%async_computation.4 | async-start | bytes 262144 | tf_op jit(solution)/shard_map/all_to_all | solution.py:79
  76.3 11.0 %all-to-all-start.5 = ((bf16[32,2,1024]{2,1,0:T(2,128)(2,1)}), bf16[32,2,1024]{2,1,0:T(2,128)(2,1)S(1)}, u32[]{:S(2)}, u32[]{:S(2)}) async-start(bf16[32,2,1024]{2,1,0:T(2,128)(2,1)} %reshape.165), calls=%async_computation.5 | async-start | bytes 262144 | tf_op jit(solution)/shard_map/all_to_all | solution.py:97
where the time goes:
time: 90 us; the launch traced here: 89.4 us
  waiting for transfers between devices  43.1 us (48%)
  starting transfers between devices  20.5 us (23%)
  local copies, waits for them, and re-layouts  18.1 us (20%)
  other arithmetic  3.66 us (4%)
  matrix products  3.42 us (4%)
    all_to_all x2, waiting for transfers between devices, on_device(): lax.all_to_all(arranged, ('row', 'col'), split_axis=1, concat_axis=0, til...  15 us
    all_to_all x2, waiting for transfers between devices, on_device(): lax.all_to_all(right_panel, ('row', 'col'), split_axis=0, concat_axis=1,...  14.6 us
    all_to_all x2, waiting for transfers between devices, on_device(): lax.all_to_all(left_panel, ('row', 'col'), split_axis=0, concat_axis=1, t...  13.6 us
    unnamed x28, local copies, waits for them, and re-layouts  10.2 us
    all_to_all x2, starting transfers between devices, on_device(): lax.all_to_all(left_panel, ('row', 'col'), split_axis=0, concat_axis=1, t...  9.9 us
    all_to_all x2, starting transfers between devices, on_device(): lax.all_to_all(right_panel, ('row', 'col'), split_axis=0, concat_axis=1,...  5.32 us
    all_to_all x2, starting transfers between devices, on_device(): lax.all_to_all(arranged, ('row', 'col'), split_axis=1, concat_axis=0, til...  5.28 us
  transfers between devices with their start and end apart: 6, of which 6 were waited for; matrix products, arithmetic and copies ran while one was open for 7% of the time, Pallas kernels for 0%

commit v1 on v0

--- a/solution.py
+++ b/solution.py
@@ -1,6 +1,10 @@
+import functools
+
 import jax
 import jax.numpy as jnp
 from jax import lax
+from jax.experimental import pallas as pl
+from jax.experimental.pallas import tpu as pltpu
 from jax.sharding import PartitionSpec as P
 
 epsilon = 1e-05
@@ -103,9 +107,315 @@
     return current.astype(jnp.bfloat16)
 
 
+MESH = pl.DeviceIdType.MESH
+F32 = jnp.float32
+BF16 = jnp.bfloat16
+
+
+def sigmoid(values):
+    return 0.5 * jnp.tanh(0.5 * values) + 0.5
+
+
+def lane_groups(shape, width):
+    return lax.broadcasted_iota(jnp.int32, shape, len(shape) - 1) // width
+
+
+def swap_groups(blocks, width):
+    count = len(blocks)
+    blocks = list(blocks)
+    lanes = count * width
+    group = lane_groups(blocks[0].shape, width)
+    step = count // 2
+    while step:
+        low = (group // step) % 2 == 0
+        for p in range(count):
+            if p & step:
+                continue
+            first, second = blocks[p], blocks[p + step]
+            shift = step * width
+            blocks[p] = jnp.where(low, first, pltpu.roll(second, shift, 1))
+            blocks[p + step] = jnp.where(low, pltpu.roll(first, lanes - shift, 1), second)
+        step //= 2
+    return blocks
+
+
+def columns_of(row_vector, lanes):
+    return jnp.transpose(jnp.broadcast_to(row_vector, (lanes, row_vector.shape[1])))
+
+
+def contract_first(left, right):
+    return lax.dot_general(left, right, (((0,), (0,)), ((), ())), preferred_element_type=F32)
+
+
+def fused_kernel(
+    row_count,
+    col_count,
+    z_ref,
+    mask_ref,
+    in_gain,
+    in_bias,
+    proj_ref,
+    gate_ref,
+    out_gain,
+    out_bias,
+    outw_ref,
+    out_ref,
+    zt_ref,
+    tmp_ref,
+    gain_ref,
+    bias_ref,
+    send1,
+    recv1,
+    send2,
+    recv2,
+    send_sem,
+    recv_sem,
+):
+    tile_rows, tile_cols, channels = z_ref.shape
+    pairs = tile_rows * tile_cols
+    devices = row_count * col_count
+    hidden = outw_ref.shape[1]
+    own = hidden // devices
+    lanes = own * tile_cols
+    blocks = pairs // lanes
+    tokens = row_count * tile_rows
+    row, col = lax.axis_index("row"), lax.axis_index("col")
+    me = row * col_count + col
+
+    def place(step):
+        target = lax.rem(me + step, devices)
+        return target, target // col_count, lax.rem(target, col_count)
+
+    barrier = pltpu.get_barrier_semaphore()
+
+    def greet(step, carry):
+        _, trow, tcol = place(step)
+        pl.semaphore_signal(barrier, inc=1, device_id=(trow, tcol), device_id_type=MESH)
+        return carry
+
+    lax.fori_loop(1, devices, greet, 0)
+
+    def copy_panels(layer, step):
+        target, trow, tcol = place(step)
+        return pltpu.make_async_remote_copy(
+            src_ref=send1.at[layer, target],
+            dst_ref=recv1.at[layer, col, row],
+            send_sem=send_sem.at[2 * layer, step],
+            recv_sem=recv_sem.at[2 * layer, step],
+            device_id=(trow, tcol),
+            device_id_type=MESH,
+        )
+
+    def copy_product(layer, step):
+        target, trow, tcol = place(step)
+        return pltpu.make_async_remote_copy(
+            src_ref=send2.at[layer, tcol, trow],
+            dst_ref=recv2.at[layer, me],
+            send_sem=send_sem.at[2 * layer + 1, step],
+            recv_sem=recv_sem.at[2 * layer + 1, step],
+            device_id=(trow, tcol),
+            device_id_type=MESH,
+        )
+
+    def start_all(make, layer):
+        def body(step, carry):
+            make(layer, step).start()
+            return carry
+
+        lax.fori_loop(1, devices, body, 0)
+
+    def arrive_all(make, layer):
+        def body(step, carry):
+            make(layer, step).wait_recv()
+            return carry
+
+        lax.fori_loop(1, devices, body, 0)
+
+    zt_ref[...] = jnp.transpose(z_ref[...].astype(F32).reshape(pairs, channels))
+    spread = (
+        lax.broadcasted_iota(jnp.int32, (tile_cols, pairs), 1) % tile_cols
+        == lax.broadcasted_iota(jnp.int32, (tile_cols, pairs), 0)
+    ).astype(F32)
+    mine = (
+        lax.broadcasted_iota(jnp.int32, (tile_rows, pairs), 1) // tile_cols
+        == lax.broadcasted_iota(jnp.int32, (tile_rows, pairs), 0)
+    ).astype(F32)
+    mask_flat = jnp.sum(
+        jnp.dot(mask_ref[...].astype(F32), spread, preferred_element_type=F32) * mine,
+        axis=0,
+        keepdims=True,
+    )
+
+    for layer in range(2):
+        current = zt_ref[...]
+        centred = current - jnp.mean(current, axis=0, keepdims=True)
+        scale = lax.rsqrt(jnp.mean(centred * centred, axis=0, keepdims=True) + epsilon)
+        gain = columns_of(in_gain[layer : layer + 1, :], lanes)
+        bias = columns_of(in_bias[layer : layer + 1, :], lanes)
+        gain = jnp.concatenate([gain] * blocks, axis=1)
+        bias = jnp.concatenate([bias] * blocks, axis=1)
+        normed = (centred * scale * gain + bias).astype(BF16)
+        projected = contract_first(proj_ref[layer], normed)
+        for side in range(2):
+            first = 2 * side * hidden
+            panel = (
+                sigmoid(projected[first : first + hidden])
+                * projected[first + hidden : first + 2 * hidden]
+                * mask_flat
+            )
+            for block in range(blocks):
+                parts = [
+                    panel[k * devices : (k + 1) * devices, block * lanes : (block + 1) * lanes]
+                    for k in range(own)
+                ]
+                for q, part in enumerate(swap_groups(parts, tile_cols)):
+                    line = block * own + q
+                    tmp_ref[side, line * devices : (line + 1) * devices, :] = part
+            for target in range(devices):
+                send1[layer, target, side] = tmp_ref[
+                    side, pl.ds(target, tile_rows, stride=devices), :
+                ].astype(BF16)
+        if layer == 0:
+            pl.semaphore_wait(barrier, devices - 1)
+        start_all(copy_panels, layer)
+        recv1[layer, col, row] = send1[layer, me]
+        gate_value = sigmoid(contract_first(gate_ref[layer], normed))
+        group = lane_groups((devices, lanes), tile_cols)
+        for source, kept in ((out_gain, gain_ref), (out_bias, bias_ref)):
+            wide = columns_of(source[layer : layer + 1, :], lanes)
+            packed = wide[0:devices]
+            for k in range(1, own):
+                packed = jnp.where(group == k, wide[k * devices : (k + 1) * devices], packed)
+            kept[...] = packed
+        arrive_all(copy_panels, layer)
+
+        left = jnp.concatenate(
+            [recv1[layer, c, :, 0].reshape(tokens, lanes) for c in range(col_count)], axis=1
+        )
+        right = jnp.concatenate(
+            [recv1[layer, c, :, 1].reshape(tokens, lanes) for c in range(col_count)], axis=1
+        )
+        if layer == 0:
+            wide_group = lane_groups((1, col_count * lanes), tile_cols) % own
+            masks = [(wide_group == k).astype(F32).astype(BF16) for k in range(own)]
+            for c in range(col_count):
+                rows = right[c * tile_cols : (c + 1) * tile_cols]
+                stacked = jnp.concatenate([rows * masks[k] for k in range(own)], axis=0)
+                product = lax.dot_general(
+                    left, stacked, (((1,), (1,)), ((), ())), preferred_element_type=F32
+                )
+                send2[layer, c] = product.astype(BF16).reshape(row_count, tile_rows, lanes)
+        else:
+            product = contract_first(left, right)
+            group = lane_groups((tile_cols, lanes), tile_cols)
+            for c in range(col_count):
+                pieces = []
+                for d in range(col_count):
+                    at = d * lanes
+                    piece = product[at : at + tile_cols, c * lanes : (c + 1) * lanes]
+                    for k in range(1, own):
+                        low = at + k * tile_cols
+                        piece = jnp.where(
+                            group == k,
+                            product[low : low + tile_cols, c * lanes : (c + 1) * lanes],
+                            piece,
+                        )
+                    pieces.append(piece.astype(BF16))
+                send2[layer, c] = jnp.concatenate(pieces, axis=0).reshape(
+                    row_count, tile_rows, lanes
+                )
+        start_all(copy_product, layer)
+        recv2[layer, me] = send2[layer, col, row]
+        arrive_all(copy_product, layer)
+
+        returned = recv2[layer].astype(F32)
+
+        def over_channels(values):
+            total = jnp.sum(values, axis=0)
+            shift = lanes // 2
+            while shift >= tile_cols:
+                total = total + pltpu.roll(total, shift, 1)
+                shift //= 2
+            return total * (1.0 / hidden)
+
+        centred = returned - over_channels(returned)[None]
+        scale = lax.rsqrt(over_channels(centred * centred) + epsilon)
+        for d in range(devices):
+            tmp_ref[0, d * tile_rows : (d + 1) * tile_rows, :] = (
+                centred[d] * scale * gain_ref[d : d + 1, :] + bias_ref[d : d + 1, :]
+            )
+        wide_blocks = []
+        for block in range(blocks):
+            parts = [
+                tmp_ref[0, pl.ds(block * own + q, devices, stride=tile_rows), :] for q in range(own)
+            ]
+            wide_blocks.append(
+                jnp.concatenate(swap_groups(parts, tile_cols), axis=0).astype(BF16)
+            )
+        update = contract_first(outw_ref[layer], jnp.concatenate(wide_blocks, axis=1))
+        zt_ref[...] = zt_ref[...] + gate_value * update
+
+    out_ref[...] = (
+        jnp.transpose(zt_ref[...]).reshape(tile_rows, tile_cols, channels).astype(BF16)
+    )
+    for layer in range(2):
+        for make in (copy_panels, copy_product):
+
+            def body(step, carry):
+                make(layer, step).wait_send()
+                return carry
+
+            lax.fori_loop(1, devices, body, 0)
+
+
+def fused(row_count, col_count, *args):
+    tile_rows, tile_cols, channels = args[0].shape
+    devices = row_count * col_count
+    hidden = args[-1].shape[1]
+    lanes = hidden // devices * tile_cols
+    pairs = tile_rows * tile_cols
+    vmem = pl.BlockSpec(memory_space=pltpu.VMEM)
+    return pl.pallas_call(
+        functools.partial(fused_kernel, row_count, col_count),
+        out_shape=jax.ShapeDtypeStruct(args[0].shape, BF16),
+        in_specs=[vmem] * len(args),
+        out_specs=vmem,
+        scratch_shapes=[
+            pltpu.VMEM((channels, pairs), F32),
+            pltpu.VMEM((2, tile_rows * devices, lanes), F32),
+            pltpu.VMEM((devices, lanes), F32),
+            pltpu.VMEM((devices, lanes), F32),
+            pltpu.VMEM((2, devices, 2, tile_rows, lanes), BF16),
+            pltpu.VMEM((2, col_count, row_count, 2, tile_rows, lanes), BF16),
+            pltpu.VMEM((2, col_count, row_count, tile_rows, lanes), BF16),
+            pltpu.VMEM((2, devices, tile_rows, lanes), BF16),
+            pltpu.SemaphoreType.DMA((4, devices)),
+            pltpu.SemaphoreType.DMA((4, devices)),
+        ],
+        compiler_params=pltpu.CompilerParams(collective_id=0, has_side_effects=True),
+    )(*args)
+
+
 def solution(mesh):
+    row_count, col_count = mesh.shape["row"], mesh.shape["col"]
+    devices = row_count * col_count
+
+    def step(*args):
+        tile_rows, tile_cols, channels = args[0].shape
+        hidden = args[-1].shape[1]
+        own = hidden // devices
+        fits = (
+            hidden % devices == 0
+            and own * tile_cols == 128
+            and tile_rows % 16 == 0
+            and tile_rows % own == 0
+            and own & (own - 1) == 0
+            and row_count * tile_rows == col_count * tile_cols
+        )
+        return fused(row_count, col_count, *args) if fits else on_device(*args)
+
     return jax.shard_map(
-        on_device,
+        step,
         mesh=mesh,
         in_specs=(P("row", "col", None), P("row", "col"), P(), P(), P(), P(), P(), P(), P()),
         out_specs=P("row", "col", None),

time: 90 us -> 43.6 us (0.48)
  waiting for transfers between devices: 43.1 us -> 0 us
  Pallas kernels: 0 us -> 41.8 us
  starting transfers between devices: 20.5 us -> 0 us
  local copies, waits for them, and re-layouts: 18.1 us -> 1.57 us
  other arithmetic: 3.66 us -> 0 us
  matrix products: 3.42 us -> 0 us
    all_to_all x6 -> x0, waiting for transfers between devices: 43.1 us -> none  [the longest x2 15 us: on_device(): lax.all_to_all(arranged, ('row', 'col'), split_axis=1, concat_axis=0, til...]
    pallas_call x0 -> x1, Pallas kernels: none -> 41.8 us  [fused(): pl.pallas_call(functools.partial(fused_kernel, row_count, col_count), out...]
    all_to_all x6 -> x0, starting transfers between devices: 20.5 us -> none  [the longest x2 9.9 us: on_device(): lax.all_to_all(left_panel, ('row', 'col'), split_axis=0, concat_axis=1, t...]
    unnamed x28 -> x1, local copies, waits for them, and re-layouts: 10.2 us -> 1.57 us
    reshape x14 -> x0, local copies, waits for them, and re-layouts: 4.23 us -> none  [the longest x2 0.82 us: on_device(): left_recv.reshape(per_device, row_count, col_count, tile_rows, tile_cols)]
    dot_general x10 -> x0, matrix products: 3.42 us -> none  [the longest x2 1.35 us: on_device(): jnp.einsum('cij,cd->ijd', normed, weight_out, preferred_element_type=jnp....]
    reduce_sum x7 -> x0, other arithmetic: 2.37 us -> none  [the longest x3 1.43 us: normalize(): average = jnp.mean(values, axis=reduce_axis, keepdims=True)]
    convert_element_type x6 -> x0, local copies, waits for them, and re-layouts: 1.83 us -> none  [the longest x4 1.72 us: gated_panel(): (jax.nn.sigmoid(projected[:hidden]) * projected[hidden:] * mask_float).as...]
  transfers between devices with their start and end apart: 6 -> 0, of which waited for: 6 -> 0; matrix products, arithmetic and copies ran while one was open for 7% -> 0% of each run, Pallas kernels for 0% -> 0%
where the time goes in v1:
time: 43.6 us; the launch traced here: 43.4 us
  Pallas kernels  41.8 us (96%)
  local copies, waits for them, and re-layouts  1.57 us (4%)
    pallas_call x1, Pallas kernels, fused(): pl.pallas_call(functools.partial(fused_kernel, row_count, col_count), out...  41.8 us
    unnamed x1, local copies, waits for them, and re-layouts  1.57 us

profile of v1, /device:TPU:0, one launch (start us, length us, event | category | flops | bytes accessed | tf_op | source)
XLA Modules:
  0.0 43.4 jit_solution(10573450090200344808)
XLA Ops:
  0.0 41.8 %shard_map.91 = bf16[16,32,128]{2,1,0:T(8,128)(2,1)} custom-call(bf16[16,32,128]{2,1,0:T(8,128)(2,1)} %z_ref.1, s32[16,32]{1,0:T(8,128)} %mask_ref.1, f32[2,128]{1,0:T(2,128)} %in_gain.1, f32[2,128]{1,0:T(2,128)} %in_bias.1, bf16[2,128,512]{2,1,0:T(8,128)(2,1)} %proj_ref.1, bf16[2,128,128]{2,1,0:T(8,128)(2,1)} %gate_ref.1, f32[2,128]{1,0:T(2,128)} %out_gain.1, ...), custom_call_target="tpu_custom_call" | custom-call | tf_op jit(solution)/shard_map/pallas_call | solution.py:378
  41.8 1.6 %copy.11 = bf16[16,32,128]{2,1,0:T(8,128)(2,1)} copy(bf16[16,32,128]{2,1,0:T(8,128)(2,1)} %shard_map.91) | data formatting | bytes 262144

commit v2 on v1

--- a/solution.py
+++ b/solution.py
@@ -150,6 +150,23 @@
 def fused_kernel(
     row_count,
     col_count,
+    *refs,
+):
+    operands, out_ref, held = refs[:9], refs[9], refs[10:19]
+    load_sem = refs[19]
+    loads = [
+        pltpu.make_async_copy(source, target, load_sem.at[at])
+        for at, (source, target) in enumerate(zip(operands, held))
+    ]
+    for at in (0, 1, 2, 3, 4, 5, 6, 7, 8):
+        loads[at].start()
+    fused_body(row_count, col_count, loads, *held, out_ref, *refs[20:])
+
+
+def fused_body(
+    row_count,
+    col_count,
+    loads,
     z_ref,
     mask_ref,
     in_gain,
@@ -182,56 +199,72 @@
     row, col = lax.axis_index("row"), lax.axis_index("col")
     me = row * col_count + col
 
-    def place(step):
-        target = lax.rem(me + step, devices)
-        return target, target // col_count, lax.rem(target, col_count)
+    half = col_count // 2
+    near, inner = col // half, lax.rem(col, half)
+
+    def place(turn, step):
+        if turn < half:
+            tcol = (1 - near) * half + lax.rem(2 * half - 1 - inner + turn, half)
+            trow = lax.rem(2 * row_count - 1 - row + step, row_count)
+        else:
+            tcol = near * half + lax.rem(inner + 1 + turn - half, half)
+            trow = lax.rem(row + 1 + step, row_count)
+        return trow * col_count + tcol, trow, tcol
+
+    def each(action):
+        for turn in range(col_count):
+
+            def body(step, carry, turn=turn):
+                action(turn, step)
+                return carry
+
+            lax.fori_loop(0, row_count - (turn == col_count - 1), body, 0, unroll=True)
 
     barrier = pltpu.get_barrier_semaphore()
 
-    def greet(step, carry):
-        _, trow, tcol = place(step)
+    def greet(turn, step):
+        _, trow, tcol = place(turn, step)
         pl.semaphore_signal(barrier, inc=1, device_id=(trow, tcol), device_id_type=MESH)
-        return carry
-
-    lax.fori_loop(1, devices, greet, 0)
-
-    def copy_panels(layer, step):
-        target, trow, tcol = place(step)
+
+    each(greet)
+
+    def copy_panels(layer, turn, step):
+        target, trow, tcol = place(turn, step)
         return pltpu.make_async_remote_copy(
             src_ref=send1.at[layer, target],
             dst_ref=recv1.at[layer, col, row],
-            send_sem=send_sem.at[2 * layer, step],
-            recv_sem=recv_sem.at[2 * layer, step],
+            send_sem=send_sem.at[2 * layer],
+            recv_sem=recv_sem.at[2 * layer],
             device_id=(trow, tcol),
             device_id_type=MESH,
         )
 
-    def copy_product(layer, step):
-        target, trow, tcol = place(step)
+    def copy_product(layer, turn, step):
+        target, trow, tcol = place(turn, step)
         return pltpu.make_async_remote_copy(
             src_ref=send2.at[layer, tcol, trow],
             dst_ref=recv2.at[layer, me],
-            send_sem=send_sem.at[2 * layer + 1, step],
-            recv_sem=recv_sem.at[2 * layer + 1, step],
+            send_sem=send_sem.at[2 * layer + 1],
+            recv_sem=recv_sem.at[2 * layer + 1],
             device_id=(trow, tcol),
             device_id_type=MESH,
         )
 
     def start_all(make, layer):
-        def body(step, carry):
-            make(layer, step).start()
-            return carry
-
-        lax.fori_loop(1, devices, body, 0)
-
-    def arrive_all(make, layer):
-        def body(step, carry):
-            make(layer, step).wait_recv()
-            return carry
-
-        lax.fori_loop(1, devices, body, 0)
-
+        each(lambda turn, step: make(layer, turn, step).start())
+
+    def wait_panels(sem, layer):
+        slots = send1.at[layer, pl.ds(0, devices - 1)]
+        pltpu.make_async_copy(slots, slots, sem.at[2 * layer]).wait()
+
+    def wait_products(sem, layer):
+        slots = recv2.at[layer, pl.ds(0, devices - 1)]
+        pltpu.make_async_copy(slots, slots, sem.at[2 * layer + 1]).wait()
+
+    loads[0].wait()
     zt_ref[...] = jnp.transpose(z_ref[...].astype(F32).reshape(pairs, channels))
+    for at in range(1, len(loads)):
+        loads[at].wait()
     spread = (
         lax.broadcasted_iota(jnp.int32, (tile_cols, pairs), 1) % tile_cols
         == lax.broadcasted_iota(jnp.int32, (tile_cols, pairs), 0)
@@ -287,7 +320,7 @@
             for k in range(1, own):
                 packed = jnp.where(group == k, wide[k * devices : (k + 1) * devices], packed)
             kept[...] = packed
-        arrive_all(copy_panels, layer)
+        wait_panels(recv_sem, layer)
 
         left = jnp.concatenate(
             [recv1[layer, c, :, 0].reshape(tokens, lanes) for c in range(col_count)], axis=1
@@ -326,7 +359,7 @@
                 )
         start_all(copy_product, layer)
         recv2[layer, me] = send2[layer, col, row]
-        arrive_all(copy_product, layer)
+        wait_products(recv_sem, layer)
 
         returned = recv2[layer].astype(F32)
 
@@ -359,13 +392,8 @@
         jnp.transpose(zt_ref[...]).reshape(tile_rows, tile_cols, channels).astype(BF16)
     )
     for layer in range(2):
-        for make in (copy_panels, copy_product):
-
-            def body(step, carry):
-                make(layer, step).wait_send()
-                return carry
-
-            lax.fori_loop(1, devices, body, 0)
+        wait_panels(send_sem, layer)
+        wait_products(send_sem, layer)
 
 
 def fused(row_count, col_count, *args):
@@ -378,9 +406,11 @@
     return pl.pallas_call(
         functools.partial(fused_kernel, row_count, col_count),
         out_shape=jax.ShapeDtypeStruct(args[0].shape, BF16),
-        in_specs=[vmem] * len(args),
+        in_specs=[pl.BlockSpec(memory_space=pl.ANY)] * len(args),
         out_specs=vmem,
-        scratch_shapes=[
+        scratch_shapes=[pltpu.VMEM(arg.shape, arg.dtype) for arg in args]
+        + [
+            pltpu.SemaphoreType.DMA((len(args),)),
             pltpu.VMEM((channels, pairs), F32),
             pltpu.VMEM((2, tile_rows * devices, lanes), F32),
             pltpu.VMEM((devices, lanes), F32),
@@ -389,8 +419,8 @@
             pltpu.VMEM((2, col_count, row_count, 2, tile_rows, lanes), BF16),
             pltpu.VMEM((2, col_count, row_count, tile_rows, lanes), BF16),
             pltpu.VMEM((2, devices, tile_rows, lanes), BF16),
-            pltpu.SemaphoreType.DMA((4, devices)),
-            pltpu.SemaphoreType.DMA((4, devices)),
+            pltpu.SemaphoreType.DMA((4,)),
+            pltpu.SemaphoreType.DMA((4,)),
         ],
         compiler_params=pltpu.CompilerParams(collective_id=0, has_side_effects=True),
     )(*args)
@@ -410,6 +440,7 @@
             and tile_rows % 16 == 0
             and tile_rows % own == 0
             and own & (own - 1) == 0
+            and col_count % 2 == 0
             and row_count * tile_rows == col_count * tile_cols
         )
         return fused(row_count, col_count, *args) if fits else on_device(*args)

time: 43.6 us -> 38.8 us (0.89)
  Pallas kernels: 41.8 us -> 37 us
    pallas_call x1, Pallas kernels: 41.8 us -> 37 us  [fused(): pl.pallas_call(functools.partial(fused_kernel, row_count, col_count), out...]
where the time goes in v2:
time: 38.8 us; the launch traced here: 38.6 us
  Pallas kernels  37 us (95%)
  local copies, waits for them, and re-layouts  1.57 us (4%)
    pallas_call x1, Pallas kernels, fused(): pl.pallas_call(functools.partial(fused_kernel, row_count, col_count), out...  37 us
    unnamed x1, local copies, waits for them, and re-layouts  1.57 us

profile of v2, /device:TPU:0, one launch (start us, length us, event | category | flops | bytes accessed | tf_op | source)
XLA Modules:
  0.0 38.6 jit_solution(9817839605650998213)
XLA Ops:
  0.0 37.0 %shard_map.91 = bf16[16,32,128]{2,1,0:T(8,128)(2,1)} custom-call(bf16[16,32,128]{2,1,0:T(8,128)(2,1)} %refs_0_.1, s32[16,32]{1,0:T(8,128)} %refs_1_.1, f32[2,128]{1,0:T(2,128)} %refs_2_.1, f32[2,128]{1,0:T(2,128)} %refs_3_.1, bf16[2,128,512]{2,1,0:T(8,128)(2,1)} %refs_4_.1, bf16[2,128,128]{2,1,0:T(8,128)(2,1)} %refs_5_.1, f32[2,128]{1,0:T(2,128)} %refs_6_.1, ...), custom_call_target="tpu_custom_call" | custom-call | tf_op jit(solution)/shard_map/pallas_call | solution.py:406
  37.0 1.6 %copy.11 = bf16[16,32,128]{2,1,0:T(8,128)(2,1)} copy(bf16[16,32,128]{2,1,0:T(8,128)(2,1)} %shard_map.91) | data formatting | bytes 262144
